TPU v7x, 128 devices: a whole 4x4x4 slice. The times are simulated.
128 devices in a mesh: ba: 16 (over y_lo, z, core), ha: 8 (over y_hi, x).
Axes of the slice: x: 4, y: 4 (y_hi: 2, y_lo: 2; y = y_hi * 2 + y_lo), z: 4, core: 2. Of those that a mesh axis runs over, the one named last changes fastest.
Arguments:
- queries: bfloat16 [4096, 64, 576], P('ba', 'ha'), may hold values from -6 to 6
- out_grad: bfloat16 [4096, 64, 512], P('ba', 'ha'), may hold values from -1.1953125 to 1.1953125
- out_saved: bfloat16 [4096, 64, 512], P('ba', 'ha'), may hold values from -3 to 3
- logsumexp: float32 [4096, 64], P('ba', 'ha'), may hold values from 7 to 9
- parents: int32 [4096], P('ba'), may hold values from 0 to 1023, as said below
- latents: bfloat16 [1024, 576], P(('ba', 'ha')), may hold values from -6 to 6
- hidden: bfloat16 [1024, 7168], P('ba', 'ha'), may hold values from -6 to 6
- latent_weight: bfloat16 [576, 7168], P(None, 'ha'), may hold values from -0.0625 to 0.0625
Outputs:
- query_grad: bfloat16 [4096, 64, 576], P('ba', 'ha')
- weight_grad: bfloat16 [576, 7168], P('ba', 'ha')
- input_grad: bfloat16 [1024, 7168], P('ba', 'ha')
Inputs may be any that keep to these rules, and one draw needn't show every extreme that they name: `parents`: the 32 tokens of each aligned block of 32 share one value; some token has 0 and some has 1023.
All inputs are finite; a program needn't handle non-finite values.
Results may differ from a plain program's by a relative error of at most 0.0067.
Values may be sent and summed in bfloat16 or wider, within the bound.
A program may use at most 64 MiB of HBM per device.

v0:
```python
import jax
import jax.numpy as jnp
from jax import lax
from jax.sharding import PartitionSpec as P

RANK = 512
ROPE = 64
softmax_scale = 192.0 ** (-0.5)


def cut_along(shard, dim, peers):
    before, after = (shard.shape[:dim], shard.shape[dim + 1 :])
    return jnp.moveaxis(shard.reshape(*before, peers, -1, *after), dim, 0)


def sent_and_summed(shard, axis, dim):
    peers = lax.axis_size(axis)
    pieces = lax.all_to_all(cut_along(shard, dim, peers), axis, 0, 0, tiled=True)
    return jnp.sum(pieces, axis=0)


def from_everyone(shard, axis):
    peers = lax.axis_size(axis)
    return lax.all_to_all(
        jnp.broadcast_to(shard[None], (peers, *shard.shape)), axis, 0, 0, tiled=True
    )


def over_copies(shard, axis):
    return from_everyone(shard, axis).sum(axis=0)


def tile_terms(query_rows, grad_rows, lse_rows, deltas, limits, key_block, offset):
    key_count = key_block.shape[0]
    key_index = offset + jnp.arange(key_count, dtype=jnp.int32)
    scores = (
        jnp.einsum("qd,kd->qk", query_rows, key_block, preferred_element_type=jnp.float32)
        * softmax_scale
    )
    visible = key_index[None, :] <= limits[:, None]
    weights = jnp.where(visible, jnp.exp(scores - lse_rows[:, None]), jnp.float32(0.0))
    grad_prob = jnp.einsum(
        "qd,kd->qk", grad_rows, key_block[:, :RANK], preferred_element_type=jnp.float32
    )
    grad_score = (weights * (grad_prob - deltas[:, None])).astype(jnp.bfloat16)
    query_part = jnp.einsum("qk,kd->qd", grad_score, key_block, preferred_element_type=jnp.float32)
    value_part = jnp.einsum(
        "qk,qd->kd", weights.astype(jnp.bfloat16), grad_rows, preferred_element_type=jnp.float32
    )
    key_grad = softmax_scale * jnp.einsum(
        "qk,qd->kd", grad_score, query_rows, preferred_element_type=jnp.float32
    )
    key_grad = key_grad + jnp.pad(value_part, ((0, 0), (0, ROPE)))
    return (query_part, key_grad)


def on_device(queries, out_grad, out_saved, logsumexp, parents, latents, hidden, latent_weight):
    tokens_here, heads_here, full_width = queries.shape
    row_total = tokens_here * heads_here
    query_rows = queries.reshape(row_total, full_width)
    grad_rows = out_grad.reshape(row_total, RANK)
    saved_rows = out_saved.reshape(row_total, RANK)
    lse_rows = logsumexp.reshape(row_total)
    limits = jnp.repeat(parents, heads_here)
    deltas = jnp.sum(saved_rows.astype(jnp.float32) * grad_rows.astype(jnp.float32), axis=1)
    all_keys = lax.all_gather(latents, ("ba", "ha"), axis=0, tiled=True)
    prefix_total = all_keys.shape[0]
    tile_len = min(256, prefix_total)
    tile_count = prefix_total // tile_len
    key_tiles = all_keys.reshape(tile_count, tile_len, full_width)
    offsets = jnp.arange(tile_count, dtype=jnp.int32) * tile_len

    def tile_step(query_acc, tile_inputs):
        key_block, offset = tile_inputs
        query_part, key_grad = tile_terms(
            query_rows, grad_rows, lse_rows, deltas, limits, key_block, offset
        )
        return (query_acc + query_part, key_grad)

    query_acc, key_stack = lax.scan(
        tile_step, jnp.zeros((row_total, full_width), jnp.float32), (key_tiles, offsets)
    )
    latent_acc = key_stack.reshape(prefix_total, full_width)
    query_grad = (
        (softmax_scale * query_acc)
        .astype(jnp.bfloat16)
        .reshape(tokens_here, heads_here, full_width)
    )
    branch_part = sent_and_summed(latent_acc, "ba", 0)
    row_grads = over_copies(branch_part, "ha").astype(jnp.bfloat16)
    weight_grad = sent_and_summed(
        jnp.einsum("pl,ph->lh", row_grads, hidden, preferred_element_type=jnp.float32), "ba", 0
    ).astype(jnp.bfloat16)
    input_grad = jnp.dot(row_grads, latent_weight, preferred_element_type=jnp.float32).astype(
        jnp.bfloat16
    )
    return (query_grad, weight_grad, input_grad)


def solution(mesh):
    return jax.shard_map(
        on_device,
        mesh=mesh,
        in_specs=(
            P("ba", "ha", None),
            P("ba", "ha", None),
            P("ba", "ha", None),
            P("ba", "ha"),
            P("ba"),
            P(("ba", "ha"), None),
            P("ba", "ha"),
            P(None, "ha"),
        ),
        out_specs=(P("ba", "ha", None), P("ba", "ha"), P("ba", "ha")),
        check_vma=False,
    )
```

profile of v0, /device:TPU:97, one launch (start us, length us, event | category | flops | bytes accessed | tf_op | source)
XLA Modules:
  0.0 485.5 jit_solution(854251680802731591)
XLA Ops:
  8.9 2.8 multiply_reduce_fusion
  11.9 5.1 %copy.20 = bf16[256,8,576]{2,1,0:T(8,128)(2,1)} copy(bf16[256,8,576]{0,2,1:T(8,128)(2,1)} %param.10) | data formatting | bytes 4718592 | tf_op args[0]
  16.9 295.1 %all-gather.2.cloned.1.call-done = bf16[1024,576]{1,0:T(8,128)(2,1)} async-done(((bf16[8,576]{1,0:T(8,128)(2,1)}), bf16[1024,576]{1,0:T(8,128)(2,1)}) %all-gather.2.cloned.1.call-update) | async-done | bytes 1179664 | tf_op jit(solution)/shard_map/all_gather | solution.py:66
  312.0 55.1 %while.16 = (s32[]{:T(128)}, f32[2048,576]{0,1:T(8,128)}, f32[4,256,576]{1,2,0:T(8,128)}, s32[4]{0:T(128)S(1)}, bf16[4,256,576]{2,1,0:T(8,128)(2,1)}, /*index=5*...) while((s32[]{:T(128)}, f32[2048,576]{0,1:T(8,128)}, ...), condition=%wide.wide.region_2.3_spmd.clone, body=%wide.wide.region_1.2_spmd.clone.sunk | while | flops 2892529920 | bytes 73387280 | solution.py:80
  314.5 2.8 fusion.69
  320.3 2.0 fusion.72
  323.7 2.1 copy-done.2
  328.2 2.8 fusion.69
  337.4 2.1 copy-done.2
  342.0 2.8 fusion.69
  347.9 2.0 fusion.72
  351.2 2.1 copy-done.2
  355.8 2.8 fusion.69
  361.7 2.0 fusion.72
  365.0 2.1 copy-done.2
  367.1 3.2 copy.23
  370.3 37.9 %all_to_all.15 = f32[16,64,576]{2,1,0:T(8,128)} all-to-all(f32[16,64,576]{2,1,0:T(8,128)} %bitcast.77), channel_id=1, replica_groups=mesh['ba'=16,'ha'=8] {'ba'}, dimensions={0} | all-to-all | bytes 4718592 | tf_op jit(solution)/shard_map/all_to_all | solution.py:18
  410.2 25.9 %all_to_all.16 = f32[8,64,576]{2,1,0:T(8,128)S(1)} all-to-all(f32[8,64,576]{2,1,0:T(8,128)S(1)} %broadcast_in_dim.34), channel_id=1, replica_groups=mesh['ba'=16,'ha'=8] {'ha'}, dimensions={0} | all-to-all | bytes 2359296 | tf_op jit(solution)/shard_map/all_to_all | solution.py:24
  438.2 5.8 %all-to-all-start.2 = ((f32[16,36,896]{2,1,0:T(8,128)}), f32[16,36,896]{2,1,0:T(8,128)}, u32[]{:S(2)}, u32[]{:S(2)}) async-start(f32[16,36,896]{2,1,0:T(8,128)} %reshape.35), calls=%async_computation.2 | async-start | bytes 4587520 | tf_op jit(solution)/shard_map/all_to_all | solution.py:18
  444.0 2.9 multiply_convert_fusion
  447.0 2.6 copy.22
  449.5 4.6 copy.24
  455.1 21.1 %all-to-all-done.2 = f32[16,36,896]{2,1,0:T(8,128)} async-done(((f32[16,36,896]{2,1,0:T(8,128)}), f32[16,36,896]{2,1,0:T(8,128)}, u32[]{:S(2)}, u32[]{:S(2)}) %all-to-all-start.2) | async-done | bytes 2064416 | tf_op jit(solution)/shard_map/all_to_all | solution.py:18
  476.2 2.4 reduce_sum.42
  (89 shorter events, 35.9 us)
Async XLA Ops:
  7.2 447.0 %copy-start = (bf16[576,896]{1,0:T(8,128)(2,1)S(1)}, bf16[576,896]{1,0:T(8,128)(2,1)}, u32[]{:S(2)}) copy-start(bf16[576,896]{1,0:T(8,128)(2,1)} %param.17) | copy-start | bytes 3096580
  7.2 304.8 %all-gather.2.cloned.1.call-start = ((), (), s32[]{:S(2)}) async-start(), calls=%async_computation.3 | async-start | bytes 1320960 | tf_op jit(solution)/shard_map/all_gather | solution.py:66
  8.8 8.1 %copy-start.4 = (f32[256,8]{1,0:T(8,128)}, f32[256,8]{1,0:T(8,128)S(1)}, u32[]{:S(2)}) copy-start(f32[256,8]{1,0:T(8,128)S(1)} %copy.21) | copy-start | bytes 24580
  11.8 300.2 %copy-start.1 = (bf16[256,8,512]{2,1,0:T(8,128)(2,1)S(1)}, bf16[256,8,512]{2,1,0:T(8,128)(2,1)}, u32[]{:S(2)}) copy-start(bf16[256,8,512]{2,1,0:T(8,128)(2,1)} %param.11) | copy-start | bytes 6291460
  11.8 300.2 %copy-start.6 = (s32[256]{0:T(256)S(1)}, s32[256]{0:T(256)}, u32[]{:S(2)}) copy-start(s32[256]{0:T(256)} %param.14) | copy-start | bytes 3076
  317.3 5.0 %slice-start = ((s8[4718592]{0:T(1024)(128)(4,1)}), s8[4194304]{0:T(1024)(128)(4,1)S(1)}, s32[]{:S(2)}) async-start(s8[4718592]{0:T(1024)(128)(4,1)} %bitcast.74), calls=%async_computation.4 | async-start | bytes 8388608 | tf_op jit(solution)/shard_map/while
  318.3 2.0 copy-start.3
  318.3 4.0 slice-start.1
  323.6 2.1 copy-start.2
  331.1 5.0 %slice-start = ((s8[4718592]{0:T(1024)(128)(4,1)}), s8[4194304]{0:T(1024)(128)(4,1)S(1)}, s32[]{:S(2)}) async-start(s8[4718592]{0:T(1024)(128)(4,1)} %bitcast.74), calls=%async_computation.4 | async-start | bytes 8388608 | tf_op jit(solution)/shard_map/while
  332.1 2.0 copy-start.3
  332.1 4.0 slice-start.1
  337.4 2.1 copy-start.2
  344.9 5.0 %slice-start = ((s8[4718592]{0:T(1024)(128)(4,1)}), s8[4194304]{0:T(1024)(128)(4,1)S(1)}, s32[]{:S(2)}) async-start(s8[4718592]{0:T(1024)(128)(4,1)} %bitcast.74), calls=%async_computation.4 | async-start | bytes 8388608 | tf_op jit(solution)/shard_map/while
  345.9 2.0 copy-start.3
  345.9 4.0 slice-start.1
  351.2 2.1 copy-start.2
  358.7 5.0 %slice-start = ((s8[4718592]{0:T(1024)(128)(4,1)}), s8[4194304]{0:T(1024)(128)(4,1)S(1)}, s32[]{:S(2)}) async-start(s8[4718592]{0:T(1024)(128)(4,1)} %bitcast.74), calls=%async_computation.4 | async-start | bytes 8388608 | tf_op jit(solution)/shard_map/while
  359.6 2.0 copy-start.3
  359.6 4.0 slice-start.1
  365.0 2.1 copy-start.2
  410.2 26.0 %copy-start.5 = (bf16[64,896]{1,0:T(8,128)(2,1)S(1)}, bf16[64,896]{1,0:T(8,128)(2,1)}, u32[]{:S(2)}) copy-start(bf16[64,896]{1,0:T(8,128)(2,1)} %param.16) | copy-start | bytes 344068
  438.2 38.0 %all-to-all-start.2 = ((f32[16,36,896]{2,1,0:T(8,128)}), f32[16,36,896]{2,1,0:T(8,128)}, u32[]{:S(2)}, u32[]{:S(2)}) async-start(f32[16,36,896]{2,1,0:T(8,128)} %reshape.35), calls=%async_computation.2 | async-start | bytes 4587520 | tf_op jit(solution)/shard_map/all_to_all | solution.py:18
Sparse Core Ops, SparseCore 0:
  9.7 302.2 all-gather.1
where the time goes:
time: 486 us; the launch traced here: 485 us
  waiting for transfers between devices  317 us (65%)
  blocking collectives  63.8 us (13%)
  local copies, waits for them, and re-layouts  38.8 us (8%)
  matrix products  32.9 us (7%)
  between operations  14.1 us (3%)
  other arithmetic  12.7 us (3%)
  starting transfers between devices  5.86 us (1%)
    all_gather x1, waiting for transfers between devices, on_device(): all_keys = lax.all_gather(latents, ('ba', 'ha'), axis=0, tiled=True)  295 us
    all_to_all x1, blocking collectives, sent_and_summed(): lax.all_to_all(cut_along(shard, dim, peers), axis, 0, 0, tiled=True)  37.9 us
    all_to_all x1, blocking collectives, from_everyone(): lax.all_to_all(jnp.broadcast_to(shard[None], (peers, *shard.shape)), axis...  25.9 us
    all_to_all x1, waiting for transfers between devices, sent_and_summed(): lax.all_to_all(cut_along(shard, dim, peers), axis, 0, 0, tiled=True)  21.1 us
    while x32, local copies, waits for them, and re-layouts  13.5 us
    dot_general x4, matrix products, tile_terms(): jnp.einsum('qd,kd->qk', query_rows, key_block, preferred_element_type=jnp...  11.4 us
    unnamed x13, local copies, waits for them, and re-layouts  10.5 us
  transfers between devices with their start and end apart: 2, of which 2 were waited for; matrix products, arithmetic and copies ran while one was open for 4% of the time, Pallas kernels for 0%

commit v1 on v0

--- a/solution.py
+++ b/solution.py
@@ -63,7 +63,10 @@
     lse_rows = logsumexp.reshape(row_total)
     limits = jnp.repeat(parents, heads_here)
     deltas = jnp.sum(saved_rows.astype(jnp.float32) * grad_rows.astype(jnp.float32), axis=1)
-    all_keys = lax.all_gather(latents, ("ba", "ha"), axis=0, tiled=True)
+    peers_2 = lax.axis_size(("ba", "ha"))
+    parts = jnp.stack([latents for _ in range(peers_2)])
+    parts = lax.all_to_all(parts, ("ba", "ha"), split_axis=0, concat_axis=0)
+    all_keys = jnp.concatenate(parts, axis=0)
     prefix_total = all_keys.shape[0]
     tile_len = min(256, prefix_total)
     tile_count = prefix_total // tile_len

time: 486 us -> 197 us (0.41)
  waiting for transfers between devices: 317 us -> 32 us
  between operations: 14.1 us -> 0.77 us
  starting transfers between devices: 5.86 us -> 16.4 us
    all_gather x1 -> x0, waiting for transfers between devices: 295 us -> none  [on_device(): all_keys = lax.all_gather(latents, ('ba', 'ha'), axis=0, tiled=True)]
    all_to_all x0 -> x1, waiting for transfers between devices: none -> 10.9 us  [on_device(): parts = lax.all_to_all(parts, ('ba', 'ha'), split_axis=0, concat_axis=0)]
    all_to_all x0 -> x1, starting transfers between devices: none -> 10.5 us  [on_device(): parts = lax.all_to_all(parts, ('ba', 'ha'), split_axis=0, concat_axis=0)]
    unnamed x13 -> x15, local copies, waits for them, and re-layouts: 10.5 us -> 9.7 us
  transfers between devices with their start and end apart: 2 -> 2, of which waited for: 2 -> 2; matrix products, arithmetic and copies ran while one was open for 4% -> 9% of each run, Pallas kernels for 0% -> 0%
where the time goes in v1:
time: 197 us; the launch traced here: 196 us
  blocking collectives  61.6 us (31%)
  local copies, waits for them, and re-layouts  40.1 us (20%)
  matrix products  32.9 us (17%)
  waiting for transfers between devices  32 us (16%)
  starting transfers between devices  16.4 us (8%)
  other arithmetic  12.1 us (6%)
    all_to_all x1, blocking collectives, sent_and_summed(): lax.all_to_all(cut_along(shard, dim, peers), axis, 0, 0, tiled=True)  37.8 us
    all_to_all x1, blocking collectives, from_everyone(): lax.all_to_all(jnp.broadcast_to(shard[None], (peers, *shard.shape)), axis...  23.8 us
    all_to_all x1, waiting for transfers between devices, sent_and_summed(): lax.all_to_all(cut_along(shard, dim, peers), axis, 0, 0, tiled=True)  21.1 us
    while x32, local copies, waits for them, and re-layouts  13.5 us
    dot_general x4, matrix products, tile_terms(): jnp.einsum('qd,kd->qk', query_rows, key_block, preferred_element_type=jnp...  11.4 us
    all_to_all x1, waiting for transfers between devices, on_device(): parts = lax.all_to_all(parts, ('ba', 'ha'), split_axis=0, concat_axis=0)  10.9 us
    all_to_all x1, starting transfers between devices, on_device(): parts = lax.all_to_all(parts, ('ba', 'ha'), split_axis=0, concat_axis=0)  10.5 us
    unnamed x15, local copies, waits for them, and re-layouts  9.7 us
  transfers between devices with their start and end apart: 2, of which 2 were waited for; matrix products, arithmetic and copies ran while one was open for 9% of the time, Pallas kernels for 0%

profile of v1, /device:TPU:97, one launch (start us, length us, event | category | flops | bytes accessed | tf_op | source)
XLA Modules:
  0.0 196.2 jit_solution(615700576185569855)
XLA Ops:
  0.7 2.1 %stack.2 = bf16[128,8,576]{2,1,0:T(8,128)(2,1)} broadcast(bf16[8,576]{1,0:T(8,128)(2,1)} %param.15), dimensions={1,2} | broadcast | bytes 1188864 | tf_op jit(solution)/shard_map/stack | solution.py:67
  2.8 10.5 %all-to-all-start = ((bf16[128,8,576]{2,1,0:T(8,128)(2,1)}), bf16[128,8,576]{2,1,0:T(8,128)(2,1)}, u32[]{:S(2)}, u32[]{:S(2)}) async-start(bf16[128,8,576]{2,1,0:T(8,128)(2,1)} %stack.2), calls=%async_computation | async-start | bytes 2621440 | tf_op jit(solution)/shard_map/all_to_all | solution.py:68
  13.6 2.2 %multiply_reduce_fusion = f32[256,8]{1,0:T(8,128)S(1)} fusion(bf16[256,8,512]{2,1,0:T(8,128)(2,1)S(1)} %copy-done.1, bf16[256,8,512]{2,1,0:T(8,128)(2,1)} %param.12), kind=kLoop, calls=%fused_computation.21 | loop fusion | flops 4192256 | bytes 4202496 | tf_op jit(solution)/shard_map/reduce_sum | solution.py:65
  15.9 4.9 %copy.20 = bf16[256,8,576]{2,1,0:T(8,128)(2,1)} copy(bf16[256,8,576]{0,2,1:T(8,128)(2,1)} %param.10) | data formatting | bytes 4718592 | tf_op args[0]
  20.9 10.9 %all-to-all-done = bf16[128,8,576]{2,1,0:T(8,128)(2,1)} async-done(((bf16[128,8,576]{2,1,0:T(8,128)(2,1)}), bf16[128,8,576]{2,1,0:T(8,128)(2,1)}, u32[]{:S(2)}, u32[]{:S(2)}) %all-to-all-start) | async-done | bytes 1179680 | tf_op jit(solution)/shard_map/all_to_all | solution.py:68
  31.7 55.1 %while.16 = (s32[]{:T(128)}, f32[2048,576]{0,1:T(8,128)}, f32[4,256,576]{1,2,0:T(8,128)}, s32[4]{0:T(128)S(1)}, bf16[4,256,576]{2,1,0:T(8,128)(2,1)}, /*index=5*...) while((s32[]{:T(128)}, f32[2048,576]{0,1:T(8,128)}, ...), condition=%wide.wide.region_2.3_spmd.clone, body=%wide.wide.region_1.2_spmd.clone.sunk | while | flops 2892529920 | bytes 73387280 | solution.py:83
  34.2 2.8 %fusion.69 = f32[2048,256]{0,1:T(8,128)S(1)} fusion(bf16[256,576]{1,0:T(8,128)(2,1)S(1)} %dynamic-slice_bitcast_fusion.3, bf16[2048,576]{1,0:T(8,128)(2,1)} %get-tuple-element.351, f32[2048]{0:T(1024)S(1)} %get-tuple-element.356, s32[2048]{0:T(1024)S(1)} %le.46, s32[256]{0:T(256)S(1)} %iota_add_fusion.3), kind=kOutput, calls=%fused_computation.9.clone.clone.1 | convolution fusion | flops 606076928 | bytes 4768768 | tf_op jit(solution)/shard_map/while/body/eval_jaxpr/qd,kd->qk/dot_general | solution.py:37
  43.4 2.1 %copy-done.2 = f32[2048,576]{0,1:T(8,128)} copy-done((f32[2048,576]{0,1:T(8,128)}, f32[2048,576]{0,1:T(8,128)S(1)}, u32[]{:S(2)}) %copy-start.2) | copy-done | bytes 4718616 | tf_op jit(solution)/shard_map/while
  47.9 2.8 %fusion.69 = f32[2048,256]{0,1:T(8,128)S(1)} fusion(bf16[256,576]{1,0:T(8,128)(2,1)S(1)} %dynamic-slice_bitcast_fusion.3, bf16[2048,576]{1,0:T(8,128)(2,1)} %get-tuple-element.351, f32[2048]{0:T(1024)S(1)} %get-tuple-element.356, s32[2048]{0:T(1024)S(1)} %le.46, s32[256]{0:T(256)S(1)} %iota_add_fusion.3), kind=kOutput, calls=%fused_computation.9.clone.clone.1 | convolution fusion | flops 606076928 | bytes 4768768 | tf_op jit(solution)/shard_map/while/body/eval_jaxpr/qd,kd->qk/dot_general | solution.py:37
  53.8 2.0 fusion.72
  57.2 2.1 %copy-done.2 = f32[2048,576]{0,1:T(8,128)} copy-done((f32[2048,576]{0,1:T(8,128)}, f32[2048,576]{0,1:T(8,128)S(1)}, u32[]{:S(2)}) %copy-start.2) | copy-done | bytes 4718616 | tf_op jit(solution)/shard_map/while
  61.7 2.8 %fusion.69 = f32[2048,256]{0,1:T(8,128)S(1)} fusion(bf16[256,576]{1,0:T(8,128)(2,1)S(1)} %dynamic-slice_bitcast_fusion.3, bf16[2048,576]{1,0:T(8,128)(2,1)} %get-tuple-element.351, f32[2048]{0:T(1024)S(1)} %get-tuple-element.356, s32[2048]{0:T(1024)S(1)} %le.46, s32[256]{0:T(256)S(1)} %iota_add_fusion.3), kind=kOutput, calls=%fused_computation.9.clone.clone.1 | convolution fusion | flops 606076928 | bytes 4768768 | tf_op jit(solution)/shard_map/while/body/eval_jaxpr/qd,kd->qk/dot_general | solution.py:37
  70.9 2.1 %copy-done.2 = f32[2048,576]{0,1:T(8,128)} copy-done((f32[2048,576]{0,1:T(8,128)}, f32[2048,576]{0,1:T(8,128)S(1)}, u32[]{:S(2)}) %copy-start.2) | copy-done | bytes 4718616 | tf_op jit(solution)/shard_map/while
  75.5 2.8 %fusion.69 = f32[2048,256]{0,1:T(8,128)S(1)} fusion(bf16[256,576]{1,0:T(8,128)(2,1)S(1)} %dynamic-slice_bitcast_fusion.3, bf16[2048,576]{1,0:T(8,128)(2,1)} %get-tuple-element.351, f32[2048]{0:T(1024)S(1)} %get-tuple-element.356, s32[2048]{0:T(1024)S(1)} %le.46, s32[256]{0:T(256)S(1)} %iota_add_fusion.3), kind=kOutput, calls=%fused_computation.9.clone.clone.1 | convolution fusion | flops 606076928 | bytes 4768768 | tf_op jit(solution)/shard_map/while/body/eval_jaxpr/qd,kd->qk/dot_general | solution.py:37
  84.7 2.1 %copy-done.2 = f32[2048,576]{0,1:T(8,128)} copy-done((f32[2048,576]{0,1:T(8,128)}, f32[2048,576]{0,1:T(8,128)S(1)}, u32[]{:S(2)}) %copy-start.2) | copy-done | bytes 4718616 | tf_op jit(solution)/shard_map/while
  86.9 3.2 %copy.23 = f32[4,256,576]{2,1,0:T(8,128)} copy(f32[4,256,576]{1,2,0:T(8,128)} %get-tuple-element.130) | data formatting | bytes 4718592 | tf_op jit(solution)/shard_map/while | solution.py:83
  90.1 37.8 %all_to_all.20 = f32[16,64,576]{2,1,0:T(8,128)} all-to-all(f32[16,64,576]{2,1,0:T(8,128)} %bitcast.77), channel_id=1, replica_groups=mesh['ba'=16,'ha'=8] {'ba'}, dimensions={0} | all-to-all | bytes 4718592 | tf_op jit(solution)/shard_map/all_to_all | solution.py:18
  129.9 23.8 %all_to_all.21 = f32[8,64,576]{2,1,0:T(8,128)S(1)} all-to-all(f32[8,64,576]{2,1,0:T(8,128)S(1)} %broadcast_in_dim.34), channel_id=1, replica_groups=mesh['ba'=16,'ha'=8] {'ha'}, dimensions={0} | all-to-all | bytes 2359296 | tf_op jit(solution)/shard_map/all_to_all | solution.py:24
  155.8 5.8 %all-to-all-start.3 = ((f32[16,36,896]{2,1,0:T(8,128)}), f32[16,36,896]{2,1,0:T(8,128)}, u32[]{:S(2)}, u32[]{:S(2)}) async-start(f32[16,36,896]{2,1,0:T(8,128)} %reshape.33), calls=%async_computation.3 | async-start | bytes 4587520 | tf_op jit(solution)/shard_map/all_to_all | solution.py:18
  161.6 2.9 %multiply_convert_fusion = bf16[2048,576]{0,1:T(8,128)(2,1)S(1)} fusion(f32[2048,576]{0,1:T(8,128)} %get-tuple-element.129), kind=kLoop, calls=%fused_computation.20 | loop fusion | flops 2359296 | bytes 7077888 | tf_op jit(solution)/shard_map/convert_element_type | solution.py:89
  164.6 2.6 %copy.22 = bf16[2048,576]{1,0:T(8,128)(2,1)} copy(bf16[2048,576]{0,1:T(8,128)(2,1)S(1)} %multiply_convert_fusion) | data formatting | bytes 4718592 | tf_op jit(solution)/shard_map/convert_element_type | solution.py:89
  167.1 4.6 %copy.24 = bf16[256,8,576]{0,2,1:T(8,128)(2,1)} copy(bf16[256,8,576]{2,1,0:T(8,128)(2,1)} %bitcast.78) | data formatting | bytes 4718592
  172.7 21.1 %all-to-all-done.3 = f32[16,36,896]{2,1,0:T(8,128)} async-done(((f32[16,36,896]{2,1,0:T(8,128)}), f32[16,36,896]{2,1,0:T(8,128)}, u32[]{:S(2)}, u32[]{:S(2)}) %all-to-all-start.3) | async-done | bytes 2064416 | tf_op jit(solution)/shard_map/all_to_all | solution.py:18
  193.8 2.4 %reduce_sum.42 = bf16[36,896]{1,0:T(8,128)(2,1)} reduce(f32[16,36,896]{2,1,0:T(8,128)} %all-to-all-done.3, f32[]{:T(128)} %constant.39.clone.1), dimensions={0}, to_apply=%region_5.6 | reduce | flops 483840 | bytes 2128900 | tf_op jit(solution)/shard_map/reduce_sum | solution.py:19
  (91 shorter events, 38.4 us)
Async XLA Ops:
  0.6 171.1 %copy-start = (bf16[576,896]{1,0:T(8,128)(2,1)S(1)}, bf16[576,896]{1,0:T(8,128)(2,1)}, u32[]{:S(2)}) copy-start(bf16[576,896]{1,0:T(8,128)(2,1)} %param.17) | copy-start | bytes 3096580
  0.6 12.7 %copy-start.7 = (f32[256,8]{0,1:T(8,128)S(1)}, f32[256,8]{0,1:T(8,128)}, u32[]{:S(2)}) copy-start(f32[256,8]{0,1:T(8,128)} %param.13) | copy-start | bytes 24580
  0.7 12.9 %copy-start.1 = (bf16[256,8,512]{2,1,0:T(8,128)(2,1)S(1)}, bf16[256,8,512]{2,1,0:T(8,128)(2,1)}, u32[]{:S(2)}) copy-start(bf16[256,8,512]{2,1,0:T(8,128)(2,1)} %param.11) | copy-start | bytes 6291460
  2.8 28.9 %all-to-all-start = ((bf16[128,8,576]{2,1,0:T(8,128)(2,1)}), bf16[128,8,576]{2,1,0:T(8,128)(2,1)}, u32[]{:S(2)}, u32[]{:S(2)}) async-start(bf16[128,8,576]{2,1,0:T(8,128)(2,1)} %stack.2), calls=%async_computation | async-start | bytes 2621440 | tf_op jit(solution)/shard_map/all_to_all | solution.py:68
  13.5 2.5 %copy-start.4 = (f32[256,8]{1,0:T(8,128)}, f32[256,8]{1,0:T(8,128)S(1)}, u32[]{:S(2)}) copy-start(f32[256,8]{1,0:T(8,128)S(1)} %copy.21) | copy-start | bytes 24580
  15.9 15.8 %copy-start.6 = (s32[256]{0:T(256)S(1)}, s32[256]{0:T(256)}, u32[]{:S(2)}) copy-start(s32[256]{0:T(256)} %param.14) | copy-start | bytes 3076
  37.0 5.0 %slice-start = ((s8[4718592]{0:T(1024)(128)(4,1)}), s8[4194304]{0:T(1024)(128)(4,1)S(1)}, s32[]{:S(2)}) async-start(s8[4718592]{0:T(1024)(128)(4,1)} %bitcast.74), calls=%async_computation.4 | async-start | bytes 8388608 | tf_op jit(solution)/shard_map/while
  38.0 2.0 %copy-start.3 = (bf16[2048,576]{1,0:T(8,128)(2,1)S(1)}, bf16[2048,576]{1,0:T(8,128)(2,1)}, u32[]{:S(2)}) copy-start(bf16[2048,576]{1,0:T(8,128)(2,1)} %get-tuple-element.351) | copy-start | bytes 7077892 | tf_op jit(solution)/shard_map/while
  38.0 4.0 %slice-start.1 = ((s8[4718592]{0:T(1024)(128)(4,1)}), s8[524288]{0:T(1024)(128)(4,1)S(1)}, s32[]{:S(2)}) async-start(s8[4718592]{0:T(1024)(128)(4,1)} %bitcast.74), calls=%async_computation.5 | async-start | bytes 1048576 | tf_op jit(solution)/shard_map/while
  43.4 2.1 %copy-start.2 = (f32[2048,576]{0,1:T(8,128)}, f32[2048,576]{0,1:T(8,128)S(1)}, u32[]{:S(2)}) copy-start(f32[2048,576]{0,1:T(8,128)S(1)} %select_add_fusion.3) | copy-start | bytes 14155780 | tf_op jit(solution)/shard_map/while
  50.8 5.0 %slice-start = ((s8[4718592]{0:T(1024)(128)(4,1)}), s8[4194304]{0:T(1024)(128)(4,1)S(1)}, s32[]{:S(2)}) async-start(s8[4718592]{0:T(1024)(128)(4,1)} %bitcast.74), calls=%async_computation.4 | async-start | bytes 8388608 | tf_op jit(solution)/shard_map/while
  51.8 2.0 %copy-start.3 = (bf16[2048,576]{1,0:T(8,128)(2,1)S(1)}, bf16[2048,576]{1,0:T(8,128)(2,1)}, u32[]{:S(2)}) copy-start(bf16[2048,576]{1,0:T(8,128)(2,1)} %get-tuple-element.351) | copy-start | bytes 7077892 | tf_op jit(solution)/shard_map/while
  51.8 4.0 %slice-start.1 = ((s8[4718592]{0:T(1024)(128)(4,1)}), s8[524288]{0:T(1024)(128)(4,1)S(1)}, s32[]{:S(2)}) async-start(s8[4718592]{0:T(1024)(128)(4,1)} %bitcast.74), calls=%async_computation.5 | async-start | bytes 1048576 | tf_op jit(solution)/shard_map/while
  57.1 2.1 %copy-start.2 = (f32[2048,576]{0,1:T(8,128)}, f32[2048,576]{0,1:T(8,128)S(1)}, u32[]{:S(2)}) copy-start(f32[2048,576]{0,1:T(8,128)S(1)} %select_add_fusion.3) | copy-start | bytes 14155780 | tf_op jit(solution)/shard_map/while
  64.6 5.0 %slice-start = ((s8[4718592]{0:T(1024)(128)(4,1)}), s8[4194304]{0:T(1024)(128)(4,1)S(1)}, s32[]{:S(2)}) async-start(s8[4718592]{0:T(1024)(128)(4,1)} %bitcast.74), calls=%async_computation.4 | async-start | bytes 8388608 | tf_op jit(solution)/shard_map/while
  65.6 2.0 %copy-start.3 = (bf16[2048,576]{1,0:T(8,128)(2,1)S(1)}, bf16[2048,576]{1,0:T(8,128)(2,1)}, u32[]{:S(2)}) copy-start(bf16[2048,576]{1,0:T(8,128)(2,1)} %get-tuple-element.351) | copy-start | bytes 7077892 | tf_op jit(solution)/shard_map/while
  65.6 4.0 %slice-start.1 = ((s8[4718592]{0:T(1024)(128)(4,1)}), s8[524288]{0:T(1024)(128)(4,1)S(1)}, s32[]{:S(2)}) async-start(s8[4718592]{0:T(1024)(128)(4,1)} %bitcast.74), calls=%async_computation.5 | async-start | bytes 1048576 | tf_op jit(solution)/shard_map/while
  70.9 2.1 %copy-start.2 = (f32[2048,576]{0,1:T(8,128)}, f32[2048,576]{0,1:T(8,128)S(1)}, u32[]{:S(2)}) copy-start(f32[2048,576]{0,1:T(8,128)S(1)} %select_add_fusion.3) | copy-start | bytes 14155780 | tf_op jit(solution)/shard_map/while
  78.4 5.0 %slice-start = ((s8[4718592]{0:T(1024)(128)(4,1)}), s8[4194304]{0:T(1024)(128)(4,1)S(1)}, s32[]{:S(2)}) async-start(s8[4718592]{0:T(1024)(128)(4,1)} %bitcast.74), calls=%async_computation.4 | async-start | bytes 8388608 | tf_op jit(solution)/shard_map/while
  79.4 2.0 %copy-start.3 = (bf16[2048,576]{1,0:T(8,128)(2,1)S(1)}, bf16[2048,576]{1,0:T(8,128)(2,1)}, u32[]{:S(2)}) copy-start(bf16[2048,576]{1,0:T(8,128)(2,1)} %get-tuple-element.351) | copy-start | bytes 7077892 | tf_op jit(solution)/shard_map/while
  79.4 4.0 %slice-start.1 = ((s8[4718592]{0:T(1024)(128)(4,1)}), s8[524288]{0:T(1024)(128)(4,1)S(1)}, s32[]{:S(2)}) async-start(s8[4718592]{0:T(1024)(128)(4,1)} %bitcast.74), calls=%async_computation.5 | async-start | bytes 1048576 | tf_op jit(solution)/shard_map/while
  84.7 2.1 %copy-start.2 = (f32[2048,576]{0,1:T(8,128)}, f32[2048,576]{0,1:T(8,128)S(1)}, u32[]{:S(2)}) copy-start(f32[2048,576]{0,1:T(8,128)S(1)} %select_add_fusion.3) | copy-start | bytes 14155780 | tf_op jit(solution)/shard_map/while
  129.9 23.9 %copy-start.5 = (bf16[64,896]{1,0:T(8,128)(2,1)S(1)}, bf16[64,896]{1,0:T(8,128)(2,1)}, u32[]{:S(2)}) copy-start(bf16[64,896]{1,0:T(8,128)(2,1)} %param.16) | copy-start | bytes 344068
  155.8 38.0 %all-to-all-start.3 = ((f32[16,36,896]{2,1,0:T(8,128)}), f32[16,36,896]{2,1,0:T(8,128)}, u32[]{:S(2)}, u32[]{:S(2)}) async-start(f32[16,36,896]{2,1,0:T(8,128)} %reshape.33), calls=%async_computation.3 | async-start | bytes 4587520 | tf_op jit(solution)/shard_map/all_to_all | solution.py:18
